TPU v7x, 32 devices: a whole 2x2x4 slice. The times are simulated.
32 devices in a mesh: row: 16 (over z, x, core), col: 2 (over y).
Axes of the slice: x: 2, y: 2, z: 4, core: 2. Of those that a mesh axis runs over, the one named last changes fastest.
Arguments:
- features: bfloat16 [16384, 512], P(('row', 'col')), may hold values from -6 to 6
- factor: float32 [16384, 1024], P(('row', 'col')), may hold values from -0.03 to 0.03
- ip_weights: float32 [16384], P(('row', 'col')), may hold values from 0.1 to 30
- pivot_owner: int32 [256], replicated, may hold values from 0 to 31, as said below
- pivot_position: int32 [256], replicated, may hold values from 0 to 511, as said below
Outputs:
- new_columns: float32 [16384, 256], P(('row', 'col'))
- gram_rows: float32 [256, 1280], replicated
Inputs may be any that keep to these rules, and one draw needn't show every extreme that they name: `pivot_owner`: each device owns at most 18 pivots, and some device owns exactly 18. `pivot_position`: pivots with the same owner have different positions.
All inputs are finite; a program needn't handle non-finite values.
Results may differ from a plain program's by a relative error of at most 0.0003.
Values may be sent and summed in bfloat16 or wider, within the bound.
No kernel may reach another device: no remote copies, remote signals or barrier semaphores. Data moves between devices by JAX's collectives and lax.ppermute only.
A program may use at most 64 MiB of HBM per device.

v0:
```python
import jax
import jax.numpy as jnp
from jax import lax
from jax.sharding import PartitionSpec as P

F = 512
kernel_rates = (0.25, 0.5, 1.0)
kernel_mixes = (0.5, 0.3, 0.2)


def kernel_of(left, right):
    cross_term = jnp.dot(left, right.T, preferred_element_type=jnp.float32)
    left_norms = jnp.sum(jnp.square(left.astype(jnp.float32)), axis=1)
    right_norms = jnp.sum(jnp.square(right.astype(jnp.float32)), axis=1)
    distance = left_norms[:, None] + right_norms[None, :] - 2.0 * cross_term
    total = jnp.zeros_like(distance)
    for rate, mixing in zip(kernel_rates, kernel_mixes):
        total = total + mixing * jnp.exp(-(rate / F) * distance)
    return total


def body(features, factor, ip_weights, pivot_owner, pivot_position):
    devices = lax.axis_size("row") * lax.axis_size("col")
    device_rank = lax.axis_index("row") * lax.axis_size("col") + lax.axis_index("col")
    pivot_count = pivot_owner.shape[0]
    slot_count = 2 * pivot_count // devices + 2
    same_owner = pivot_owner[:, None] == pivot_owner[None, :]
    earlier = jnp.arange(pivot_count)[None, :] < jnp.arange(pivot_count)[:, None]
    slot_rank = jnp.sum((same_owner & earlier).astype(jnp.int32), axis=1)
    chosen = (pivot_owner == device_rank)[None, :] & (
        slot_rank[None, :] == jnp.arange(slot_count)[:, None]
    )
    filled = jnp.any(chosen, axis=1)[:, None]
    slot_rows = jnp.sum(jnp.where(chosen, pivot_position[None, :], 0), axis=1)
    slot_x = jnp.where(filled, features[slot_rows], jnp.zeros((), jnp.bfloat16))
    slot_h = jnp.where(filled, factor[slot_rows], 0.0)
    every_x = lax.all_gather(slot_x, ("row", "col"), axis=0, tiled=True)
    every_h = lax.all_gather(slot_h, ("row", "col"), axis=0, tiled=True)
    source = pivot_owner * slot_count + slot_rank
    pivot_x = every_x[source]
    pivot_h = every_h[source]
    residual = kernel_of(features, pivot_x) - jnp.dot(
        factor, pivot_h.T, precision=lax.Precision.HIGHEST
    )
    block = kernel_of(pivot_x, pivot_x) - jnp.dot(
        pivot_h, pivot_h.T, precision=lax.Precision.HIGHEST
    )
    lower_block = jnp.linalg.cholesky(block)
    new_columns = jax.scipy.linalg.solve_triangular(lower_block, residual.T, lower=True).T
    weighted = new_columns * ip_weights[:, None]
    left_part = jnp.dot(weighted.T, factor, precision=lax.Precision.HIGHEST)
    right_part = jnp.dot(weighted.T, new_columns, precision=lax.Precision.HIGHEST)
    local_gram = jnp.concatenate([left_part, right_part], axis=1)
    summed = lax.psum(local_gram, ("row", "col"))
    total_samples = features.shape[0] * devices
    return (new_columns, summed / total_samples)


def solution(mesh):
    placed = (P(("row", "col"), None), P(("row", "col"), None), P(("row", "col")), P(), P())
    return jax.shard_map(
        body, mesh=mesh, in_specs=placed, out_specs=(P(("row", "col"), None), P()), check_vma=False
    )
```

profile of v0, /device:TPU:0, one launch (start us, length us, event | category | flops | bytes accessed | tf_op | source)
XLA Modules:
  0.0 309.8 jit_solution(2607362890105495387)
XLA Ops:
  7.2 1.0 convert_reduce_fusion
  8.3 0.7 broadcast_compare_fusion
  9.1 0.8 select_reduce_fusion.2
  9.9 0.6 gather_fusion.2
  10.5 0.7 select_bitcast_fusion
  11.3 1.7 gather_fusion
  13.1 75.1 %all-gather = bf16[32,18,512]{2,1,0:T(8,128)(2,1)S(1)} all-gather(bf16[1,18,512]{2,1,0:T(8,128)(2,1)S(1)} %select_bitcast_fusion.2), channel_id=1, replica_groups=mesh['row'=16,'col'=2] {'row','col'}, dimensions={0}, use_global_device_ids=true | all-gather | bytes 608256 | tf_op jit(solution)/shard_map/all_gather | solution.py:37
  88.4 1.2 gather_fusion.1
  89.8 0.8 copy.23
  91.0 1.1 fusion
  92.1 3.1 reshape.102
  95.2 3.2 %gather_fusion.3 = f32[256,1024]{1,0:T(8,128)S(1)} fusion(f32[576,1024]{1,0:T(8,128)} %reshape.102, s32[1024]{0:T(1024)S(1)} %pad_clamp_fusion), kind=kCustom, calls=%fused_computation.3 | custom fusion | bytes 2098176 | tf_op jit(solution)/shard_map/gather | solution.py:41
  98.4 1.7 fusion.26
  100.1 2.9 convolution_subtract_fusion
  103.0 1.1 copy.24
  104.1 1.5 fusion.9
  105.6 11.7 %cholesky.50 = f32[128,128]{1,0:T(8,128)S(1)} custom-call(f32[128,128]{1,0:T(8,128)S(1)} %cholesky.118), custom_call_target="Cholesky" | custom-call | tf_op jit(solution)/shard_map/jit(cholesky)/cholesky | solution.py:48
  117.4 9.8 %custom-call.15 = f32[1,128,128]{1,2,0:T(8,128)S(1)} custom-call(f32[1,128,128]{2,1,0:T(8,128)S(1)} %get-tuple-element.31), custom_call_target="InvertDiagBlocksLowerTriangular" | custom-call | tf_op jit(solution)/shard_map/jit(cholesky)/cholesky | solution.py:48
  127.7 11.9 %cholesky.105 = f32[128,128]{1,0:T(8,128)S(1)} custom-call(f32[128,128]{1,0:T(8,128)S(1)} %convolution_subtract_fusion.2), custom_call_target="Cholesky" | custom-call | tf_op jit(solution)/shard_map/jit(cholesky)/cholesky | solution.py:48
  139.6 0.7 compare_reduce_fusion
  141.8 5.3 %while.1 = (s32[]{:T(128)}, f32[256,256]{1,0:T(8,128)S(1)}, s32[2,2]{1,0:T(2,128)S(1)}, f32[2,128,128]{2,1,0:T(8,128)}, s32[]{:T(128)}) while((s32[]{:T(128)}, f32[256,256]{1,0:T(8,128)S(1)}, s32[2,2]{1,0:T(2,128)S(1)}, f32[2,128,128]{2,1,0:T(8,128)}, s32[]{:T(128)}) %tuple.31), condition=%wide.while_cond, body=%wide.while_body.sunk | while | flops 2 | bytes 132205 | solution.py:49
  141.8 0.6 fusion.41
  142.4 2.0 bitcast_dynamic-update-slice_fusion.2
  144.5 0.6 fusion.41
  145.1 2.0 bitcast_dynamic-update-slice_fusion.2
  147.1 20.5 %custom-call.16 = f32[2,128,128]{1,2,0:T(8,128)S(1)} custom-call(f32[2,128,128]{2,1,0:T(8,128)} %get-tuple-element.9), custom_call_target="InvertDiagBlocksLowerTriangular" | custom-call | tf_op jit(solution)/shard_map/jit(_solve_triangular)/triangular_solve | solution.py:49
  168.9 0.6 fusion.1
  169.5 1.9 fusion.3
  171.4 1.2 pad_maximum_fusion
  172.6 1.0 copy.26
  173.6 126.9 %all-reduce.3.cloned.1.call-done = f32[256,1280]{1,0:T(8,128)} async-done(((f32[256,1280]{1,0:T(8,128)}), f32[256,1280]{1,0:T(8,128)}) %all-reduce.3.cloned.1.call-update) | async-done | bytes 1310736 | tf_op jit(solution)/shard_map/psum | solution.py:54
  300.5 2.5 broadcast_multiply_fusion
  (47 shorter events, 3.1 us)
Async XLA Ops:
  7.2 2.7 copy-start
  7.2 81.2 %copy-start.6 = (s32[256]{0:T(256)S(1)}, s32[256]{0:T(256)}, u32[]{:S(2)}) copy-start(s32[256]{0:T(256)} %param.8) | copy-start | bytes 3076
  7.2 84.9 %all-gather.4.cloned.1.call-start = ((), (), s32[]{:S(2)}) async-start(), calls=%async_computation.1 | async-start | bytes 3244032 | tf_op jit(solution)/shard_map/all_gather | solution.py:38
  11.2 289.3 %all-reduce.3.cloned.1.call-start = ((), (), s32[]{:S(2)}) async-start(), calls=%async_computation | async-start | bytes 2621440 | tf_op jit(solution)/shard_map/psum | solution.py:54
  88.3 2.5 copy-start.1
  89.8 2.3 copy-start.2
  98.4 1.7 copy-start.5
  100.1 4.0 %copy-start.3 = (f32[256,256]{0,1:T(8,128)S(1)}, f32[256,256]{0,1:T(8,128)}, u32[]{:S(2)}) copy-start(f32[256,256]{0,1:T(8,128)} %copy-done.2) | copy-start | bytes 786436
  104.1 63.5 %copy-start.4 = (f32[256,512]{1,0:T(8,128)S(1)}, f32[256,512]{1,0:T(8,128)}, u32[]{:S(2)}) copy-start(f32[256,512]{1,0:T(8,128)} %convolution_subtract_fusion) | copy-start | bytes 1572868
  117.4 51.5 %copy-start.7 = (f32[512]{0:T(512)S(1)}, f32[512]{0:T(512)}, u32[]{:S(2)}) copy-start(f32[512]{0:T(512)} %param.7) | copy-start | bytes 6148
Sparse Core Ops, SparseCore 0:
  11.5 63.7 all-gather.3
  172.7 127.7 all-reduce.2
where the time goes:
time: 310 us
  waiting for transfers between devices  127 us (41%)
  blocking collectives  75.1 us (24%)
  other arithmetic  63.6 us (21%)
  local copies, waits for them, and re-layouts  18.3 us (6%)
  between operations  15.7 us (5%)
  matrix products  10.2 us (3%)
    psum x1, waiting for transfers between devices, body(): summed = lax.psum(local_gram, ('row', 'col'))  127 us
    all_gather x1, blocking collectives, body(): every_x = lax.all_gather(slot_x, ('row', 'col'), axis=0, tiled=True)  75.1 us
    another operation x6, other arithmetic, body(): lower_block = jnp.linalg.cholesky(block)  34.2 us
    another operation x3, other arithmetic, body(): jax.scipy.linalg.solve_triangular(lower_block, residual.T, lower=True)  20.5 us
  transfers between devices with their start and end apart: 2, of which 1 were waited for; matrix products, arithmetic and copies ran while one was open for 2% of the time, Pallas kernels for 0%

commit v1 on v0

--- a/solution.py
+++ b/solution.py
@@ -51,7 +51,9 @@
     left_part = jnp.dot(weighted.T, factor, precision=lax.Precision.HIGHEST)
     right_part = jnp.dot(weighted.T, new_columns, precision=lax.Precision.HIGHEST)
     local_gram = jnp.concatenate([left_part, right_part], axis=1)
-    summed = lax.psum(local_gram, ("row", "col"))
+    summed = local_gram
+    for name in ("col", "row"):
+        summed = lax.psum(summed, name)
     total_samples = features.shape[0] * devices
     return (new_columns, summed / total_samples)
 

time: 310 us -> 321 us (1.035)
  waiting for transfers between devices: 127 us -> 138 us
    psum x1 -> x2, waiting for transfers between devices: 127 us -> 138 us  [body(): summed = lax.psum(summed, name)]
  transfers between devices with their start and end apart: 2 -> 3, of which waited for: 1 -> 2; matrix products, arithmetic and copies ran while one was open for 2% -> 2% of each run, Pallas kernels for 0% -> 0%
where the time goes in v1:
time: 321 us
  waiting for transfers between devices  138 us (43%)
  blocking collectives  75.1 us (23%)
  other arithmetic  63.6 us (20%)
  local copies, waits for them, and re-layouts  18.3 us (6%)
  between operations  15.4 us (5%)
  matrix products  10.2 us (3%)
    psum x2, waiting for transfers between devices, body(): summed = lax.psum(summed, name)  138 us
    all_gather x1, blocking collectives, body(): every_x = lax.all_gather(slot_x, ('row', 'col'), axis=0, tiled=True)  75.1 us
    another operation x6, other arithmetic, body(): lower_block = jnp.linalg.cholesky(block)  34.2 us
    another operation x3, other arithmetic, body(): jax.scipy.linalg.solve_triangular(lower_block, residual.T, lower=True)  20.5 us
  transfers between devices with their start and end apart: 3, of which 2 were waited for; matrix products, arithmetic and copies ran while one was open for 2% of the time, Pallas kernels for 0%

profile of v1, /device:TPU:0, one launch (start us, length us, event | category | flops | bytes accessed | tf_op | source)
XLA Modules:
  0.0 321.0 jit_solution(2771996350621624352)
XLA Ops:
  7.2 1.0 convert_reduce_fusion
  8.3 0.7 broadcast_compare_fusion
  9.1 0.8 select_reduce_fusion.2
  10.5 0.7 select_bitcast_fusion
  11.3 1.7 gather_fusion
  13.1 75.1 %all-gather = bf16[32,18,512]{2,1,0:T(8,128)(2,1)S(1)} all-gather(bf16[1,18,512]{2,1,0:T(8,128)(2,1)S(1)} %select_bitcast_fusion.2), channel_id=1, replica_groups=mesh['row'=16,'col'=2] {'row','col'}, dimensions={0}, use_global_device_ids=true | all-gather | bytes 608256 | tf_op jit(solution)/shard_map/all_gather | solution.py:37
  88.4 1.2 gather_fusion.1
  89.8 0.8 copy.23
  91.0 1.1 fusion
  92.1 3.1 reshape.102
  95.2 3.2 %gather_fusion.3 = f32[256,1024]{1,0:T(8,128)S(1)} fusion(f32[576,1024]{1,0:T(8,128)} %reshape.102, s32[1024]{0:T(1024)S(1)} %pad_clamp_fusion), kind=kCustom, calls=%fused_computation.3 | custom fusion | bytes 2098176 | tf_op jit(solution)/shard_map/gather | solution.py:41
  98.4 1.7 fusion.26
  100.1 2.9 convolution_subtract_fusion
  103.0 1.1 copy.24
  104.1 1.5 fusion.9
  105.6 11.7 %cholesky.50 = f32[128,128]{1,0:T(8,128)S(1)} custom-call(f32[128,128]{1,0:T(8,128)S(1)} %cholesky.118), custom_call_target="Cholesky" | custom-call | tf_op jit(solution)/shard_map/jit(cholesky)/cholesky | solution.py:48
  117.4 9.8 %custom-call.15 = f32[1,128,128]{1,2,0:T(8,128)S(1)} custom-call(f32[1,128,128]{2,1,0:T(8,128)S(1)} %get-tuple-element.31), custom_call_target="InvertDiagBlocksLowerTriangular" | custom-call | tf_op jit(solution)/shard_map/jit(cholesky)/cholesky | solution.py:48
  127.7 11.9 %cholesky.105 = f32[128,128]{1,0:T(8,128)S(1)} custom-call(f32[128,128]{1,0:T(8,128)S(1)} %convolution_subtract_fusion.2), custom_call_target="Cholesky" | custom-call | tf_op jit(solution)/shard_map/jit(cholesky)/cholesky | solution.py:48
  139.6 0.7 compare_reduce_fusion
  141.8 5.3 %while.1 = (s32[]{:T(128)}, f32[256,256]{1,0:T(8,128)S(1)}, s32[2,2]{1,0:T(2,128)S(1)}, f32[2,128,128]{2,1,0:T(8,128)}, s32[]{:T(128)}) while((s32[]{:T(128)}, f32[256,256]{1,0:T(8,128)S(1)}, s32[2,2]{1,0:T(2,128)S(1)}, f32[2,128,128]{2,1,0:T(8,128)}, s32[]{:T(128)}) %tuple.31), condition=%wide.while_cond, body=%wide.while_body.sunk | while | flops 2 | bytes 132205 | solution.py:49
  141.8 0.6 fusion.41
  142.4 2.0 bitcast_dynamic-update-slice_fusion.2
  144.5 0.6 fusion.41
  145.1 2.0 bitcast_dynamic-update-slice_fusion.2
  147.1 20.5 %custom-call.16 = f32[2,128,128]{1,2,0:T(8,128)S(1)} custom-call(f32[2,128,128]{2,1,0:T(8,128)} %get-tuple-element.9), custom_call_target="InvertDiagBlocksLowerTriangular" | custom-call | tf_op jit(solution)/shard_map/jit(_solve_triangular)/triangular_solve | solution.py:49
  168.9 0.6 fusion.1
  169.5 1.9 fusion.3
  171.4 1.2 pad_maximum_fusion
  172.6 41.8 %all-reduce.4.cloned.1.call-done = f32[256,1280]{1,0:T(8,128)} async-done(((f32[256,1280]{1,0:T(8,128)}), f32[256,1280]{1,0:T(8,128)}) %all-reduce.4.cloned.1.call-update) | async-done | bytes 1310736 | tf_op jit(solution)/shard_map/psum | solution.py:56
  214.5 1.0 copy.26
  215.5 96.6 %all-reduce.6.cloned.1.call-done = f32[256,1280]{1,0:T(8,128)} async-done(((f32[256,1280]{1,0:T(8,128)}), f32[256,1280]{1,0:T(8,128)}) %all-reduce.6.cloned.1.call-update) | async-done | bytes 1310736 | tf_op jit(solution)/shard_map/psum | solution.py:56
  312.1 2.5 broadcast_multiply_fusion
  (50 shorter events, 3.7 us)
Async XLA Ops:
  7.2 2.7 copy-start
  7.2 81.2 %copy-start.6 = (s32[256]{0:T(256)S(1)}, s32[256]{0:T(256)}, u32[]{:S(2)}) copy-start(s32[256]{0:T(256)} %param.8) | copy-start | bytes 3076
  7.2 84.9 %all-gather.4.cloned.1.call-start = ((), (), s32[]{:S(2)}) async-start(), calls=%async_computation.2 | async-start | bytes 3244032 | tf_op jit(solution)/shard_map/all_gather | solution.py:38
  11.2 203.2 %all-reduce.4.cloned.1.call-start = ((), (), s32[]{:S(2)}) async-start(), calls=%async_computation | async-start | bytes 2621440 | tf_op jit(solution)/shard_map/psum | solution.py:56
  88.3 2.5 copy-start.1
  89.8 2.3 copy-start.2
  98.4 1.7 copy-start.5
  100.1 4.0 %copy-start.3 = (f32[256,256]{0,1:T(8,128)S(1)}, f32[256,256]{0,1:T(8,128)}, u32[]{:S(2)}) copy-start(f32[256,256]{0,1:T(8,128)} %copy-done.2) | copy-start | bytes 786436
  104.1 63.5 %copy-start.4 = (f32[256,512]{1,0:T(8,128)S(1)}, f32[256,512]{1,0:T(8,128)}, u32[]{:S(2)}) copy-start(f32[256,512]{1,0:T(8,128)} %convolution_subtract_fusion) | copy-start | bytes 1572868
  117.4 51.5 %copy-start.7 = (f32[512]{0:T(512)S(1)}, f32[512]{0:T(512)}, u32[]{:S(2)}) copy-start(f32[512]{0:T(512)} %param.7) | copy-start | bytes 6148
  172.6 139.5 %all-reduce.6.cloned.1.call-start = ((), (), s32[]{:S(2)}) async-start(), calls=%async_computation.1 | async-start | bytes 2621440 | tf_op jit(solution)/shard_map/psum | solution.py:56
Sparse Core Ops, SparseCore 0:
  11.5 63.7 all-gather.3
  172.7 41.6 all-reduce.3
  217.9 94.1 all-reduce.5
